TPU v7x, 32 devices: a whole 2x2x4 slice. The times are simulated.
32 devices in a mesh: dp: 8 (over y, x, core), mp: 4 (over z).
Axes of the slice: x: 2, y: 2, z: 4, core: 2. Of those that a mesh axis runs over, the one named last changes fastest.
Arguments:
- patches: bfloat16 [24576, 3072], P(('dp', 'mp')), may hold values from -6 to 6
- wavelengths: int32 [12], replicated, may hold values from 400 to 2499
- counts: int32 [384], P('dp'), may hold values from 1 to 64, 18432 in all
- positions: int32 [384, 64], P(('dp', 'mp')), may hold values from 0 to 195, as said below
- relation: bfloat16 [128, 384], replicated, may hold values from -1 to 1
- blending: bfloat16 [128, 128], replicated, may hold values from -0.5 to 0.5
- widening: bfloat16 [128, 2048], replicated, may hold values from -0.5 to 0.5
- narrowing: bfloat16 [2048, 128], replicated, may hold values from -0.125 to 0.125
- generator: bfloat16 [256, 128, 768], P(('dp', 'mp')), may hold values from -0.009765625 to 0.009765625
- shifting: bfloat16 [128, 768], replicated, may hold values from -0.5 to 0.5
- scaling: bfloat16 [768], replicated, may hold values from 0.25 to 1.75
- centring: bfloat16 [768], replicated, may hold values from -1.5 to 1.5
- attending: bfloat16 [768, 3, 768], P(None, None, 'mp'), may hold values from -0.21875 to 0.21875
- offsets: bfloat16 [2, 768], P(None, 'mp'), may hold values from -1.5 to 1.5
- merging: bfloat16 [768, 768], P('mp'), may hold values from -0.875 to 0.875
- lifting: bfloat16 [768], replicated, may hold values from -1.5 to 1.5
- rescaling: bfloat16 [768], replicated, may hold values from 0.25 to 1.75
- recentring: bfloat16 [768], replicated, may hold values from -1.5 to 1.5
- expanding: bfloat16 [768, 3072], P(None, 'mp'), may hold values from -0.21875 to 0.21875
- priming: bfloat16 [3072], P('mp'), may hold values from -1.5 to 1.5
- shrinking: bfloat16 [3072, 768], P('mp'), may hold values from -0.109375 to 0.109375
- settling: bfloat16 [768], replicated, may hold values from -1.5 to 1.5
- cotangent: bfloat16 [24576, 768], P(('dp', 'mp')), may hold values from -6 to 6
Outputs:
- layer_out: bfloat16 [24576, 768], P(('dp', 'mp'))
- patches_grad: float32 [24576, 3072], P(('dp', 'mp'))
- relation_grad: float32 [128, 384], replicated
- blending_grad: float32 [128, 128], replicated
- widening_grad: float32 [128, 2048], replicated
- narrowing_grad: float32 [2048, 128], replicated
- generator_grad: float32 [256, 128, 768], P(('dp', 'mp'))
- shifting_grad: float32 [128, 768], replicated
- scaling_grad: float32 [768], replicated
- centring_grad: float32 [768], replicated
- attending_grad: float32 [768, 3, 768], P(None, None, 'mp')
- offsets_grad: float32 [2, 768], P(None, 'mp')
- merging_grad: float32 [768, 768], P('mp')
- lifting_grad: float32 [768], replicated
- rescaling_grad: float32 [768], replicated
- recentring_grad: float32 [768], replicated
- expanding_grad: float32 [768, 3072], P(None, 'mp')
- priming_grad: float32 [3072], P('mp')
- shrinking_grad: float32 [3072, 768], P('mp')
- settling_grad: float32 [768], replicated
Inputs may be any that keep to these rules, and one draw needn't show every extreme that they name: Image i keeps its first counts[i] slots; the counts of all images sum to 18432, and some image keeps all 64. The 64 positions of an image are distinct cells of its 14 x 14 grid of patches.
All inputs are finite; a program needn't handle non-finite values. No bound on the sum of `counts` on one device may be relied on, other than what follows from the above.
Results may differ from a plain program's by a relative error of at most 0.025.
Values may be sent and summed in bfloat16 or wider, within the bound.
A program may use at most 192 MiB of HBM per device.

v0:
```python
from functools import partial
import jax
import jax.numpy as jnp
from jax import lax
from jax.sharding import PartitionSpec as P

HEADS = 12
HYP_HEADS = 4
GRID_SIDE = 14


def normalize(values, epsilon):
    center = values - jnp.mean(values, axis=-1, keepdims=True)
    return center * lax.rsqrt(jnp.mean(center * center, axis=-1, keepdims=True) + epsilon)


def norm_parts(values, epsilon):
    center = values - jnp.mean(values, axis=-1, keepdims=True)
    inverse = lax.rsqrt(jnp.mean(center * center, axis=-1, keepdims=True) + epsilon)
    return (center * inverse, inverse)


def norm_backward(upstream, normed_rows, inverse, gain_row):
    scaled = upstream * gain_row
    return inverse * (
        scaled
        - jnp.mean(scaled, axis=-1, keepdims=True)
        - normed_rows * jnp.mean(scaled * normed_rows, axis=-1, keepdims=True)
    )


def wave_embed(wavelengths, columns):
    halfway = columns // 2
    omegas = 10000.0 ** (-jnp.arange(halfway, dtype=jnp.float32) / halfway)
    angles = wavelengths.astype(jnp.float32)[:, None] * 0.01 * omegas[None, :]
    return jnp.concatenate([jnp.sin(angles), jnp.cos(angles)], axis=1)


def place_embed(positions, columns):
    quarter = columns // 4
    omegas = 10000.0 ** (-jnp.arange(quarter, dtype=jnp.float32) / quarter)
    across = (positions // GRID_SIDE).astype(jnp.float32)[..., None] * omegas
    upward = (positions % GRID_SIDE).astype(jnp.float32)[..., None] * omegas
    return jnp.concatenate(
        [jnp.sin(across), jnp.cos(across), jnp.sin(upward), jnp.cos(upward)], axis=-1
    )


def hyper_forward(wavelengths, relation, blending, widening, narrowing, shifting):
    highest = lax.Precision.HIGHEST
    columns = relation.shape[0]
    head_size = columns // HYP_HEADS
    embedded = wave_embed(wavelengths, columns)
    joined = jnp.dot(embedded, relation, precision=highest).reshape(
        embedded.shape[0], 3, HYP_HEADS, head_size
    )
    scores = jnp.einsum(
        "bhd,chd->hbc", joined[:, 0], joined[:, 1], precision=highest
    ) * head_size ** (-0.5)
    weights = jax.nn.softmax(scores, axis=-1)
    context = jnp.einsum("hbc,chd->bhd", weights, joined[:, 2], precision=highest).reshape(
        embedded.shape[0], columns
    )
    settled = normalize(embedded + jnp.dot(context, blending, precision=highest), 1e-05)
    widened = jax.nn.gelu(jnp.dot(settled, widening, precision=highest), approximate=False)
    hyper_out = normalize(settled + jnp.dot(widened, narrowing, precision=highest), 1e-05)
    bias_embed = jnp.dot(jnp.mean(hyper_out, axis=0), shifting, precision=highest)
    return (hyper_out, bias_embed)


def body(
    patches,
    wavelengths,
    counts,
    positions,
    relation,
    blending,
    widening,
    narrowing,
    generator,
    shifting,
    scaling,
    centring,
    attending,
    offsets,
    merging,
    lifting,
    rescaling,
    recentring,
    expanding,
    priming,
    shrinking,
    settling,
    cotangent,
):
    highest = lax.Precision.HIGHEST
    single = jnp.float32
    narrow = jnp.bfloat16
    local_rows = patches.shape[0]
    own_images = positions.shape[0]
    slot_count = positions.shape[1]
    model_width = merging.shape[1]
    local_width = merging.shape[0]
    head_size = model_width // HEADS
    local_heads = local_width // head_size
    score_scale = head_size ** (-0.5)
    my_index = lax.axis_index("mp")
    own_counts = lax.dynamic_slice_in_dim(counts, my_index * own_images, own_images)
    group_images = counts.shape[0]
    group_rows = group_images * slot_count
    hyper_params = tuple(
        (weight.astype(single) for weight in (relation, blending, widening, narrowing, shifting))
    )
    (hyper_out, bias_embed), hyper_pullback = jax.vjp(
        partial(hyper_forward, wavelengths), *hyper_params
    )
    hyper_low = hyper_out.astype(narrow)
    kernel_part = jnp.einsum(
        "ch,phd->pcd", hyper_low, generator, preferred_element_type=single
    ).astype(narrow)
    piece_rows = kernel_part.shape[0] * kernel_part.shape[1]
    kernel_whole = lax.all_gather(
        kernel_part.reshape(piece_rows, model_width), ("dp", "mp"), axis=0, tiled=True
    )
    embedded = jnp.dot(patches, kernel_whole, preferred_element_type=single)
    kept_rows = (
        (jnp.arange(slot_count)[None, :] < own_counts[:, None])
        .astype(single)
        .reshape(local_rows, 1)
    )
    start_rows = (
        place_embed(positions, model_width).reshape(local_rows, model_width) + bias_embed + embedded
    )
    first_hat, first_inverse = norm_parts(start_rows, 1e-06)
    first_normed = (first_hat * scaling.astype(single) + centring.astype(single)).astype(narrow)
    first_all = lax.all_gather(first_normed, "mp", axis=0, tiled=True)
    attend_flat = attending.reshape(model_width, 3 * local_width)
    attend_bias = jnp.concatenate(
        [offsets[0].astype(single), jnp.zeros((local_width,), single), offsets[1].astype(single)]
    )
    joined = (jnp.dot(first_all, attend_flat, preferred_element_type=single) + attend_bias).astype(
        narrow
    )
    split_shape = (group_images, slot_count, local_heads, head_size)
    queries = joined[:, :local_width].reshape(split_shape)
    keys_all = joined[:, local_width : 2 * local_width].reshape(split_shape)
    values = joined[:, 2 * local_width :].reshape(split_shape)
    keys_valid = (jnp.arange(slot_count)[None, :] < counts[:, None])[:, None, None, :]

    def score_block(query_rows, key_rows):
        raw_scores = (
            jnp.einsum("ishd,ithd->ihst", query_rows, key_rows, preferred_element_type=single)
            * score_scale
        )
        return jnp.where(keys_valid, raw_scores, -1000000000.0)

    scores = score_block(queries, keys_all)
    highest_score = jnp.max(scores, axis=-1, keepdims=True)
    log_total = highest_score + jnp.log(
        jnp.sum(jnp.exp(scores - highest_score), axis=-1, keepdims=True)
    )
    attention = jnp.exp(scores - log_total)
    context = (
        jnp.einsum(
            "ihst,ithd->ishd", attention.astype(narrow), values, preferred_element_type=single
        )
        .astype(narrow)
        .reshape(group_rows, local_width)
    )
    attended = lax.psum_scatter(
        jnp.dot(context, merging, preferred_element_type=single).astype(jnp.bfloat16),
        "mp",
        scatter_dimension=0,
        tiled=True,
    ).astype(jnp.float32)
    middle = start_rows + attended + lifting.astype(single)
    second_hat, second_inverse = norm_parts(middle, 1e-06)
    second_normed = (second_hat * rescaling.astype(single) + recentring.astype(single)).astype(
        narrow
    )
    second_all = lax.all_gather(second_normed, "mp", axis=0, tiled=True)
    widened = jnp.dot(second_all, expanding, preferred_element_type=single) + priming.astype(single)
    hidden = jax.nn.gelu(widened, approximate=False).astype(narrow)
    shrunk = lax.psum_scatter(
        jnp.dot(hidden, shrinking, preferred_element_type=single).astype(jnp.bfloat16),
        "mp",
        scatter_dimension=0,
        tiled=True,
    ).astype(jnp.float32)
    result = middle + shrunk + settling.astype(single)
    layer_out = (result * kept_rows).astype(narrow)
    out_grad = cotangent.astype(single) * kept_rows
    settling_grad = jnp.sum(out_grad, axis=0)
    out_all = lax.all_gather(out_grad.astype(narrow), "mp", axis=0, tiled=True)
    shrinking_grad = jnp.einsum("gf,gd->fd", hidden, out_all, preferred_element_type=single)
    hidden_grad = jnp.einsum("gd,fd->gf", out_all, shrinking, preferred_element_type=single)
    gelu_pullback = jax.vjp(partial(jax.nn.gelu, approximate=False), widened)[1]
    widened_grad = gelu_pullback(hidden_grad)[0].astype(narrow)
    priming_grad = jnp.sum(widened_grad, axis=0, dtype=single)
    expanding_grad = jnp.einsum(
        "gd,gf->df", second_all, widened_grad, preferred_element_type=single
    )
    second_grad = lax.psum_scatter(
        jnp.einsum("gf,df->gd", widened_grad, expanding, preferred_element_type=single).astype(
            jnp.bfloat16
        ),
        "mp",
        scatter_dimension=0,
        tiled=True,
    ).astype(jnp.float32)
    rescaling_grad = jnp.sum(second_grad * second_hat, axis=0)
    recentring_grad = jnp.sum(second_grad, axis=0)
    middle_grad = out_grad + norm_backward(
        second_grad, second_hat, second_inverse, rescaling.astype(single)
    )
    lifting_grad = jnp.sum(middle_grad, axis=0)
    middle_all = lax.all_gather(middle_grad.astype(narrow), "mp", axis=0, tiled=True)
    merging_grad = jnp.einsum("gc,gd->cd", context, middle_all, preferred_element_type=single)
    context_grad = (
        jnp.einsum("gd,cd->gc", middle_all, merging, preferred_element_type=single)
        .astype(narrow)
        .reshape(split_shape)
    )
    attention = jnp.exp(score_block(queries, keys_all) - log_total)
    attention_grad = jnp.einsum(
        "ishd,ithd->ihst", context_grad, values, preferred_element_type=single
    )
    values_grad = jnp.einsum(
        "ihst,ishd->ithd", attention.astype(narrow), context_grad, preferred_element_type=single
    ).astype(narrow)
    scores_grad = (
        attention * (attention_grad - jnp.sum(attention * attention_grad, axis=-1, keepdims=True))
    ).astype(narrow)
    queries_grad = (
        jnp.einsum("ihst,ithd->ishd", scores_grad, keys_all, preferred_element_type=single)
        * score_scale
    ).astype(narrow)
    keys_grad = (
        jnp.einsum("ihst,ishd->ithd", scores_grad, queries, preferred_element_type=single)
        * score_scale
    ).astype(narrow)
    joined_grad = jnp.concatenate(
        [
            queries_grad.reshape(group_rows, local_width),
            keys_grad.reshape(group_rows, local_width),
            values_grad.reshape(group_rows, local_width),
        ],
        axis=1,
    )
    attending_grad = jnp.einsum(
        "gd,gc->dc", first_all, joined_grad, preferred_element_type=single
    ).reshape(model_width, 3, local_width)
    offsets_grad = jnp.stack(
        [
            jnp.sum(joined_grad[:, :local_width], axis=0, dtype=single),
            jnp.sum(joined_grad[:, 2 * local_width :], axis=0, dtype=single),
        ]
    )
    first_grad = lax.psum_scatter(
        jnp.einsum("gc,dc->gd", joined_grad, attend_flat, preferred_element_type=single).astype(
            jnp.bfloat16
        ),
        "mp",
        scatter_dimension=0,
        tiled=True,
    ).astype(jnp.float32)
    scaling_grad = jnp.sum(first_grad * first_hat, axis=0)
    centring_grad = jnp.sum(first_grad, axis=0)
    start_grad = middle_grad + norm_backward(
        first_grad, first_hat, first_inverse, scaling.astype(single)
    )
    shift_total = jnp.sum(start_grad, axis=0)
    start_low = start_grad.astype(narrow)
    patches_grad = jnp.einsum("rd,kd->rk", start_low, kernel_whole, preferred_element_type=single)
    kernel_grad = lax.psum_scatter(
        jnp.einsum("rk,rd->kd", patches, start_low, preferred_element_type=single),
        ("dp", "mp"),
        scatter_dimension=0,
        tiled=True,
    ).reshape(kernel_part.shape)
    generator_grad = jnp.einsum(
        "ch,pcd->phd", hyper_low.astype(single), kernel_grad, precision=highest
    )
    hyper_part = jnp.einsum("pcd,phd->ch", kernel_grad, generator.astype(single), precision=highest)
    (
        scaling_grad,
        centring_grad,
        rescaling_grad,
        recentring_grad,
        lifting_grad,
        settling_grad,
        shift_total,
        hyper_part,
    ) = lax.psum(
        (
            scaling_grad,
            centring_grad,
            rescaling_grad,
            recentring_grad,
            lifting_grad,
            settling_grad,
            shift_total,
            hyper_part,
        ),
        ("dp", "mp"),
    )
    relation_grad, blending_grad, widening_grad, narrowing_grad, shifting_grad = hyper_pullback(
        (hyper_part, shift_total)
    )
    attending_grad, offsets_grad, merging_grad, expanding_grad, priming_grad, shrinking_grad = (
        lax.psum(
            (
                attending_grad,
                offsets_grad,
                merging_grad,
                expanding_grad,
                priming_grad,
                shrinking_grad,
            ),
            "dp",
        )
    )
    return (
        layer_out,
        patches_grad,
        relation_grad,
        blending_grad,
        widening_grad,
        narrowing_grad,
        generator_grad,
        shifting_grad,
        scaling_grad,
        centring_grad,
        attending_grad,
        offsets_grad,
        merging_grad,
        lifting_grad,
        rescaling_grad,
        recentring_grad,
        expanding_grad,
        priming_grad,
        shrinking_grad,
        settling_grad,
    )


def solution(mesh):
    placed = (
        P(("dp", "mp"), None),
        P(),
        P("dp"),
        P(("dp", "mp"), None),
        P(),
        P(),
        P(),
        P(),
        P(("dp", "mp"), None, None),
        P(),
        P(),
        P(),
        P(None, None, "mp"),
        P(None, "mp"),
        P("mp", None),
        P(),
        P(),
        P(),
        P(None, "mp"),
        P("mp"),
        P("mp", None),
        P(),
        P(("dp", "mp"), None),
    )
    return jax.shard_map(
        body,
        mesh=mesh,
        in_specs=placed,
        out_specs=(
            P(("dp", "mp"), None),
            P(("dp", "mp"), None),
            P(),
            P(),
            P(),
            P(),
            P(("dp", "mp"), None, None),
            P(),
            P(),
            P(),
            P(None, None, "mp"),
            P(None, "mp"),
            P("mp", None),
            P(),
            P(),
            P(),
            P(None, "mp"),
            P("mp"),
            P("mp", None),
            P(),
        ),
        check_vma=False,
    )
```

profile of v0, /device:TPU:0, one launch (start us, length us, event | category | flops | bytes accessed | tf_op | source)
XLA Modules:
  0.0 1249.0 jit_solution(4035318917937270795)
XLA Ops:
  23.8 60.3 %all-gather.6.cloned.1.call-done = bf16[3072,768]{1,0:T(8,128)(2,1)} async-done(((bf16[96,768]{1,0:T(8,128)(2,1)}), bf16[3072,768]{1,0:T(8,128)(2,1)}) %all-gather.6.cloned.1.call-update) | async-done | bytes 4718608 | tf_op jit(solution)/shard_map/all_gather | solution.py:122
  84.1 7.9 fusion.111
  96.2 87.1 %all-gather.8.cloned.1.call-done = bf16[3072,768]{0,1:T(8,128)(2,1)} async-done(((bf16[768,768]{0,1:T(8,128)(2,1)}), bf16[3072,768]{0,1:T(8,128)(2,1)}) %all-gather.8.cloned.1.call-update) | async-done | bytes 4718608 | tf_op jit(solution)/shard_map/all_gather | solution.py:136
  231.3 83.2 %reduce-scatter.8.cloned.1.call-done = bf16[768,768]{0,1:T(8,128)(2,1)} async-done(((bf16[3072,768]{0,1:T(8,128)(2,1)}), bf16[768,768]{0,1:T(8,128)(2,1)}) %reduce-scatter.8.cloned.1.call-update) | async-done | bytes 1179664 | tf_op jit(solution)/shard_map/reduce_scatter | solution.py:170
  322.8 86.9 %all-gather.10.cloned.1.call-done = bf16[3072,768]{0,1:T(8,128)(2,1)} async-done(((bf16[768,768]{0,1:T(8,128)(2,1)}), bf16[3072,768]{0,1:T(8,128)(2,1)}) %all-gather.10.cloned.1.call-update) | async-done | bytes 4718608 | tf_op jit(solution)/shard_map/all_gather | solution.py:181
  409.7 10.7 fusion.112
  420.4 79.2 %all-gather.12.cloned.1.call-done = bf16[3072,768]{0,1:T(8,128)(2,1)} async-done(((bf16[768,768]{0,1:T(8,128)(2,1)}), bf16[3072,768]{0,1:T(8,128)(2,1)}) %all-gather.12.cloned.1.call-update) | async-done | bytes 4718608 | tf_op jit(solution)/shard_map/all_gather | solution.py:194
  499.5 28.5 %convert_reduce_fusion = (f32[768]{0:T(1024)S(1)}, bf16[3072,768]{1,0:T(8,128)(2,1)S(1)}, f32[3072,768]{1,0:T(8,128)}) fusion(f32[3072,768]{1,0:T(8,128)} %fusion.112, f32[768]{0:T(1024)S(1)} %convert_element_type.192, bf16[3072,768]{0,1:T(8,128)(2,1)} %all-gather.12.cloned.1.call-done, bf16[768,768]{1,0:T(8,128)(2,1)} %param.43), kind=kOutput, calls=%fused_computation.2 | convolution fusion | flops 3800825088 | bytes 29497344 | tf_op jit(solution)/shard_map/gd,fd->gf/dot_general | solution.py:196
  536.0 10.8 multiply_convert_fusion
  546.8 8.8 convolution_convert_fusion.1
  556.2 63.3 %reduce-scatter.12.cloned.1.call-done = bf16[768,768]{0,1:T(8,128)(2,1)} async-done(((bf16[3072,768]{0,1:T(8,128)(2,1)}), bf16[768,768]{0,1:T(8,128)(2,1)}) %reduce-scatter.12.cloned.1.call-update) | async-done | bytes 1179664 | tf_op jit(solution)/shard_map/reduce_scatter | solution.py:203
  622.6 85.7 %reduce-scatter.10.cloned.1.call-done = bf16[768,768]{0,1:T(8,128)(2,1)} async-done(((bf16[3072,768]{0,1:T(8,128)(2,1)}), bf16[768,768]{0,1:T(8,128)(2,1)}) %reduce-scatter.10.cloned.1.call-update) | async-done | bytes 1179664 | tf_op jit(solution)/shard_map/reduce_scatter | solution.py:184
  715.1 90.0 %all-gather.14.cloned.1.call-done = bf16[3072,768]{0,1:T(8,128)(2,1)} async-done(((bf16[768,768]{0,1:T(8,128)(2,1)}), bf16[3072,768]{0,1:T(8,128)(2,1)}) %all-gather.14.cloned.1.call-update) | async-done | bytes 4718608 | tf_op jit(solution)/shard_map/all_gather | solution.py:217
  864.6 7.5 convolution_convert_fusion.2
  872.4 83.6 %reduce-scatter.14.cloned.1.call-done = bf16[768,768]{0,1:T(8,128)(2,1)} async-done(((bf16[3072,768]{0,1:T(8,128)(2,1)}), bf16[768,768]{0,1:T(8,128)(2,1)}) %reduce-scatter.14.cloned.1.call-update) | async-done | bytes 1179664 | tf_op jit(solution)/shard_map/reduce_scatter | solution.py:259
  963.1 8.5 convolution_bitcast_fusion
  971.6 9.6 copy.144
  982.0 9.0 fusion.115
  991.0 9.5 fusion.116
  1003.1 14.6 %all-reduce.4 = (f32[2,192]{1,0:T(2,128)}, f32[768]{0:T(1024)}) all-reduce(f32[2,192]{1,0:T(2,128)S(1)} %pad_maximum_fusion.2, f32[768]{0:T(1024)S(1)} %get-tuple-element.102), channel_id=1, replica_groups=mesh['dp'=8,'mp'=4] {'dp'}, use_global_device_ids=true, to_apply=%region_38.39 | all-reduce | flops 1152 | bytes 9216 | tf_op jit(solution)/shard_map/psum | solution.py:311
  1030.8 8.8 fusion.35
  1039.7 78.7 %reduce-scatter.16.cloned.1.call-done = f32[96,768]{1,0:T(8,128)} async-done(((f32[3072,768]{1,0:T(8,128)}), f32[96,768]{1,0:T(8,128)}) %reduce-scatter.16.cloned.1.call-update) | async-done | bytes 294928 | tf_op jit(solution)/shard_map/reduce_scatter | solution.py:275
  1120.7 41.7 %all-reduce.3 = (f32[12,128]{1,0:T(8,128)S(1)}, f32[768]{0:T(1024)S(1)}, f32[768]{0:T(1024)}, f32[768]{0:T(1024)}, f32[768]{0:T(1024)}, /*index=5*/f32[768]{0:T(1024)}, f32[768]{0:T(1024)}, f32[768]{0:T(1024)}) all-reduce(f32[12,128]{1,0:T(8,128)S(1)} %convolution_bitcast_fusion.6, ...), channel_id=1, replica_groups=mesh['dp'=8,'mp'=4] {'dp','mp'}, use_global_device_ids=true, to_apply=%region_23.24 | all-reduce | flops 6912 | bytes 55296 | tf_op jit(solution)/shard_map/psum | solution.py:294
  1183.0 52.6 %all-reduce.8.cloned.1.call-done = (f32[768,3,192]{0,2,1:T(8,128)}, f32[192,768]{1,0:T(8,128)}, f32[768,768]{1,0:T(8,128)}, f32[768,768]{1,0:T(8,128)}) async-done(((f32[768,3,192]{0,2,1:T(8,128)}, f32[192,768]{1,0:T(8,128)}, f32[768,768]{1,0:T(8,128)}, f32[768,768]{1,0:T(8,128)}), (f32[768,3,192]{0,2,1:T(8,128)}, f32[192,768]{1,0:T(8,128)}, f32[768,768]{1,0:T(8,128)}, ...) | async-done | bytes 7077904 | tf_op jit(solution)/shard_map/psum | solution.py:311
  (329 shorter events, 207.2 us)
Async XLA Ops:
  7.2 76.9 %all-gather.6.cloned.1.call-start = ((), (), s32[]{:S(2)}) async-start(), calls=%async_computation.5 | async-start | bytes 4866048 | tf_op jit(solution)/shard_map/all_gather | solution.py:122
  17.6 165.6 %all-gather.8.cloned.1.call-start = ((), (), s32[]{:S(2)}) async-start(), calls=%async_computation.6 | async-start | bytes 5898240 | tf_op jit(solution)/shard_map/all_gather | solution.py:136
  95.4 219.0 %reduce-scatter.8.cloned.1.call-start = ((), (), s32[]{:S(2)}) async-start(), calls=%async_computation.7 | async-start | bytes 5898240 | tf_op jit(solution)/shard_map/reduce_scatter | solution.py:170
  230.6 179.1 %all-gather.10.cloned.1.call-start = ((), (), s32[]{:S(2)}) async-start(), calls=%async_computation.8 | async-start | bytes 5898240 | tf_op jit(solution)/shard_map/all_gather | solution.py:181
  319.6 179.9 %all-gather.12.cloned.1.call-start = ((), (), s32[]{:S(2)}) async-start(), calls=%async_computation.10 | async-start | bytes 5898240 | tf_op jit(solution)/shard_map/all_gather | solution.py:194
  322.8 296.8 %reduce-scatter.12.cloned.1.call-start = ((), (), s32[]{:S(2)}) async-start(), calls=%async_computation.11 | async-start | bytes 5898240 | tf_op jit(solution)/shard_map/reduce_scatter | solution.py:203
  535.7 172.6 %reduce-scatter.10.cloned.1.call-start = ((), (), s32[]{:S(2)}) async-start(), calls=%async_computation.9 | async-start | bytes 5898240 | tf_op jit(solution)/shard_map/reduce_scatter | solution.py:184
  555.6 249.6 %all-gather.14.cloned.1.call-start = ((), (), s32[]{:S(2)}) async-start(), calls=%async_computation.12 | async-start | bytes 5898240 | tf_op jit(solution)/shard_map/all_gather | solution.py:217
  715.1 241.0 %reduce-scatter.14.cloned.1.call-start = ((), (), s32[]{:S(2)}) async-start(), calls=%async_computation.13 | async-start | bytes 5898240 | tf_op jit(solution)/shard_map/reduce_scatter | solution.py:259
  872.2 246.2 %reduce-scatter.16.cloned.1.call-start = ((), (), s32[]{:S(2)}) async-start(), calls=%async_computation.14 | async-start | bytes 9732096 | tf_op jit(solution)/shard_map/reduce_scatter | solution.py:275
  981.3 254.3 %all-reduce.8.cloned.1.call-start = ((), (), s32[]{:S(2)}) async-start(), calls=%async_computation.15 | async-start | bytes 14155776 | tf_op jit(solution)/shard_map/psum | solution.py:311
  1030.7 131.7 %copy-start.21 = (bf16[128,768]{1,0:T(8,128)(2,1)S(1)}, bf16[128,768]{1,0:T(8,128)(2,1)}, u32[]{:S(2)}) copy-start(bf16[128,768]{1,0:T(8,128)(2,1)} %param.32) | copy-start | bytes 589828
  1030.7 131.9 %copy-start.25 = (f32[12,128]{1,0:T(8,128)S(1)}, f32[12,128]{1,0:T(8,128)}, u32[]{:S(2)}) copy-start(f32[12,128]{1,0:T(8,128)} %copy-done.24) | copy-start | bytes 18436
  1030.7 131.9 %copy-start.54 = (f32[12]{0:T(128)S(1)}, f32[12]{0:T(128)}, u32[]{:S(2)}) copy-start(f32[12]{0:T(128)} %copy-done.53) | copy-start | bytes 148
  1030.7 132.1 %copy-start.77 = (f32[12]{0:T(128)S(1)}, f32[12]{0:T(128)}, u32[]{:S(2)}) copy-start(f32[12]{0:T(128)} %copy-done.76) | copy-start | bytes 148
  1030.7 132.2 %copy-start.58 = (f32[12]{0:T(128)S(1)}, f32[12]{0:T(128)}, u32[]{:S(2)}) copy-start(f32[12]{0:T(128)} %copy-done.57) | copy-start | bytes 148
  1030.8 132.4 %copy-start.37 = (f32[12,2048]{1,0:T(8,128)S(1)}, f32[12,2048]{1,0:T(8,128)}, u32[]{:S(2)}) copy-start(f32[12,2048]{1,0:T(8,128)} %copy-done.36) | copy-start | bytes 294916
  1039.6 125.3 %copy-start.56 = (f32[12]{0:T(128)S(1)}, f32[12]{0:T(128)}, u32[]{:S(2)}) copy-start(f32[12]{0:T(128)} %copy-done.55) | copy-start | bytes 148
  1039.6 126.0 %copy-start.75 = (f32[12]{0:T(128)S(1)}, f32[12]{0:T(128)}, u32[]{:S(2)}) copy-start(f32[12]{0:T(128)} %copy-done.74) | copy-start | bytes 148
  1039.6 126.0 %copy-start.63 = (f32[12]{0:T(128)S(1)}, f32[12]{0:T(128)}, u32[]{:S(2)}) copy-start(f32[12]{0:T(128)} %copy-done.62) | copy-start | bytes 148
  1039.6 126.2 %copy-start.50 = (bf16[128,128]{1,0:T(8,128)(2,1)S(1)}, bf16[128,128]{1,0:T(8,128)(2,1)}, u32[]{:S(2)}) copy-start(bf16[128,128]{1,0:T(8,128)(2,1)} %param.28) | copy-start | bytes 98308
  1039.6 126.5 %copy-start.29 = (f32[4,12,12]{1,2,0:T(8,128)S(1)}, f32[4,12,12]{1,2,0:T(8,128)}, u32[]{:S(2)}) copy-start(f32[4,12,12]{1,2,0:T(8,128)} %copy-done.28) | copy-start | bytes 6916
  1039.6 126.5 %copy-start.35 = (f32[12,1,4,32]{3,2,1,0:T(4,128)S(1)}, f32[12,1,4,32]{3,2,1,0:T(4,128)}, u32[]{:S(2)}) copy-start(f32[12,1,4,32]{3,2,1,0:T(4,128)} %copy-done.34) | copy-start | bytes 18436
  1039.6 126.5 %copy-start.52 = (f32[4,12]{1,0:T(4,128)S(1)}, f32[4,12]{1,0:T(4,128)}, u32[]{:S(2)}) copy-start(f32[4,12]{1,0:T(4,128)} %copy-done.51) | copy-start | bytes 580
  (72 other events, 1021.6 us)
Sparse Core Ops, SparseCore 0:
  17.7 66.2 all-gather.5
  95.5 87.6 all-gather.7
  230.7 83.6 reduce-scatter.7
  319.8 89.8 all-gather.9
  411.7 87.7 all-gather.11
  535.8 83.6 reduce-scatter.11
  622.4 85.7 reduce-scatter.9
  715.2 89.9 all-gather.13
  872.3 83.6 reduce-scatter.13
  981.4 136.9 reduce-scatter.15
  1123.2 112.3 all-reduce.7
where the time goes:
time: 1260 us; the launch traced here: 1250 us
  waiting for transfers between devices  851 us (68%)
  matrix products  171 us (14%)
  local copies, waits for them, and re-layouts  110 us (9%)
  blocking collectives  56.3 us (4%)
  other arithmetic  44.2 us (4%)
  between operations  15.2 us (1%)
    all_gather x1, waiting for transfers between devices, body(): lax.all_gather(middle_grad.astype(narrow), 'mp', axis=0, tiled=True)  90 us
    all_gather x1, waiting for transfers between devices, body(): first_all = lax.all_gather(first_normed, 'mp', axis=0, tiled=True)  87.1 us
    all_gather x1, waiting for transfers between devices, body(): second_all = lax.all_gather(second_normed, 'mp', axis=0, tiled=True)  86.9 us
    reduce_scatter x1, waiting for transfers between devices, body(): lax.psum_scatter(jnp.dot(hidden, shrinking, preferred_element_type=single...  85.7 us
    reduce_scatter x1, waiting for transfers between devices, body(): lax.psum_scatter(jnp.einsum('gc,dc->gd', joined_grad, attend_flat, prefer...  83.6 us
    reduce_scatter x1, waiting for transfers between devices, body(): lax.psum_scatter(jnp.dot(context, merging, preferred_element_type=single)...  83.2 us
    all_gather x1, waiting for transfers between devices, body(): out_all = lax.all_gather(out_grad.astype(narrow), 'mp', axis=0, tiled=True)  79.2 us
    reduce_scatter x1, waiting for transfers between devices, body(): lax.psum_scatter(jnp.einsum('rk,rd->kd', patches, start_low, preferred_el...  78.7 us
  transfers between devices with their start and end apart: 11, of which 11 were waited for; matrix products, arithmetic and copies ran while one was open for 9% of the time, Pallas kernels for 0%

commit v1 on v0

--- a/solution.py
+++ b/solution.py
@@ -133,7 +133,15 @@
     )
     first_hat, first_inverse = norm_parts(start_rows, 1e-06)
     first_normed = (first_hat * scaling.astype(single) + centring.astype(single)).astype(narrow)
-    first_all = lax.all_gather(first_normed, "mp", axis=0, tiled=True)
+    ways, here = (lax.axis_size("mp"), lax.axis_index("mp"))
+    grown, reach = (first_normed, 1)
+    while reach < ways:
+        theirs = lax.ppermute(grown, "mp", [(d, d ^ reach) for d in range(ways)])
+        mine_first = jnp.concatenate([grown, theirs], axis=0)
+        theirs_first = jnp.concatenate([theirs, grown], axis=0)
+        grown = jnp.where(here & reach == 0, mine_first, theirs_first)
+        reach = 2 * reach
+    first_all = grown
     attend_flat = attending.reshape(model_width, 3 * local_width)
     attend_bias = jnp.concatenate(
         [offsets[0].astype(single), jnp.zeros((local_width,), single), offsets[1].astype(single)]

time: 1260 us -> 1310 us (1.040)
  waiting for transfers between devices: 851 us -> 889 us
    ppermute x0 -> x2, waiting for transfers between devices: none -> 129 us  [body(): theirs = lax.ppermute(grown, 'mp', [(d, d ^ reach) for d in range(ways)])]
    all_gather x1 -> x0, waiting for transfers between devices: 87.1 us -> none  [body(): first_all = lax.all_gather(first_normed, 'mp', axis=0, tiled=True)]
    unnamed x180 -> x178, local copies, waits for them, and re-layouts: 42.6 us -> 42.2 us
  transfers between devices with their start and end apart: 11 -> 12, of which waited for: 11 -> 12; matrix products, arithmetic and copies ran while one was open for 9% -> 8% of each run, Pallas kernels for 0% -> 0%
where the time goes in v1:
time: 1310 us; the launch traced here: 1300 us
  waiting for transfers between devices  889 us (68%)
  matrix products  175 us (13%)
  local copies, waits for them, and re-layouts  110 us (8%)
  blocking collectives  56.4 us (4%)
  other arithmetic  46.5 us (4%)
  between operations  15.4 us (1%)
    ppermute x2, waiting for transfers between devices, body(): theirs = lax.ppermute(grown, 'mp', [(d, d ^ reach) for d in range(ways)])  129 us
    all_gather x1, waiting for transfers between devices, body(): lax.all_gather(middle_grad.astype(narrow), 'mp', axis=0, tiled=True)  90 us
    all_gather x1, waiting for transfers between devices, body(): second_all = lax.all_gather(second_normed, 'mp', axis=0, tiled=True)  86.7 us
    reduce_scatter x1, waiting for transfers between devices, body(): lax.psum_scatter(jnp.dot(hidden, shrinking, preferred_element_type=single...  85.5 us
    reduce_scatter x1, waiting for transfers between devices, body(): lax.psum_scatter(jnp.einsum('gc,dc->gd', joined_grad, attend_flat, prefer...  83.6 us
    reduce_scatter x1, waiting for transfers between devices, body(): lax.psum_scatter(jnp.dot(context, merging, preferred_element_type=single)...  83.1 us
    all_gather x1, waiting for transfers between devices, body(): out_all = lax.all_gather(out_grad.astype(narrow), 'mp', axis=0, tiled=True)  79.2 us
    reduce_scatter x1, waiting for transfers between devices, body(): lax.psum_scatter(jnp.einsum('rk,rd->kd', patches, start_low, preferred_el...  75.9 us
  transfers between devices with their start and end apart: 12, of which 12 were waited for; matrix products, arithmetic and copies ran while one was open for 8% of the time, Pallas kernels for 0%

profile of v1, /device:TPU:0, one launch (start us, length us, event | category | flops | bytes accessed | tf_op | source)
XLA Modules:
  0.0 1296.4 jit_solution(1468726410651737585)
XLA Ops:
  23.8 60.3 %all-gather.5.cloned.1.call-done = bf16[3072,768]{1,0:T(8,128)(2,1)} async-done(((bf16[96,768]{1,0:T(8,128)(2,1)}), bf16[3072,768]{1,0:T(8,128)(2,1)}) %all-gather.5.cloned.1.call-update) | async-done | bytes 4718608 | tf_op jit(solution)/shard_map/all_gather | solution.py:122
  95.3 26.8 %collective-permute-done = bf16[768,768]{0,1:T(8,128)(2,1)} collective-permute-done((bf16[768,768]{0,1:T(8,128)(2,1)S(1)}, bf16[768,768]{0,1:T(8,128)(2,1)}, u32[]{:S(2)}, u32[]{:S(2)}) %collective-permute-start) | collective-permute-done | bytes 1179680 | tf_op jit(solution)/shard_map/ppermute | solution.py:139
  127.2 102.5 %collective-permute-done.1 = bf16[1536,768]{0,1:T(8,128)(2,1)} collective-permute-done((bf16[1536,768]{0,1:T(8,128)(2,1)}, bf16[1536,768]{0,1:T(8,128)(2,1)}, u32[]{:S(2)}, u32[]{:S(2)}) %collective-permute-start.1) | collective-permute-done | bytes 2359328 | tf_op jit(solution)/shard_map/ppermute | solution.py:139
  279.4 83.1 %reduce-scatter.8.cloned.1.call-done = bf16[768,768]{0,1:T(8,128)(2,1)} async-done(((bf16[3072,768]{0,1:T(8,128)(2,1)}), bf16[768,768]{0,1:T(8,128)(2,1)}) %reduce-scatter.8.cloned.1.call-update) | async-done | bytes 1179664 | tf_op jit(solution)/shard_map/reduce_scatter | solution.py:178
  371.1 86.7 %all-gather.7.cloned.1.call-done = bf16[3072,768]{0,1:T(8,128)(2,1)} async-done(((bf16[768,768]{0,1:T(8,128)(2,1)}), bf16[3072,768]{0,1:T(8,128)(2,1)}) %all-gather.7.cloned.1.call-update) | async-done | bytes 4718608 | tf_op jit(solution)/shard_map/all_gather | solution.py:189
  457.8 10.7 fusion.115
  468.4 79.2 %all-gather.9.cloned.1.call-done = bf16[3072,768]{0,1:T(8,128)(2,1)} async-done(((bf16[768,768]{0,1:T(8,128)(2,1)}), bf16[3072,768]{0,1:T(8,128)(2,1)}) %all-gather.9.cloned.1.call-update) | async-done | bytes 4718608 | tf_op jit(solution)/shard_map/all_gather | solution.py:202
  547.6 28.5 %convert_reduce_fusion = (f32[768]{0:T(1024)S(1)}, bf16[3072,768]{1,0:T(8,128)(2,1)S(1)}, f32[3072,768]{1,0:T(8,128)}) fusion(f32[3072,768]{1,0:T(8,128)} %fusion.115, f32[768]{0:T(1024)S(1)} %convert_element_type.192, bf16[3072,768]{0,1:T(8,128)(2,1)} %all-gather.9.cloned.1.call-done, bf16[768,768]{1,0:T(8,128)(2,1)} %param.43), kind=kOutput, calls=%fused_computation.2 | convolution fusion | flops 3800825088 | bytes 29497344 | tf_op jit(solution)/shard_map/gd,fd->gf/dot_general | solution.py:204
  584.2 10.8 multiply_convert_fusion
  595.0 8.8 convolution_convert_fusion.1
  604.5 63.2 %reduce-scatter.12.cloned.1.call-done = bf16[768,768]{0,1:T(8,128)(2,1)} async-done(((bf16[3072,768]{0,1:T(8,128)(2,1)}), bf16[768,768]{0,1:T(8,128)(2,1)}) %reduce-scatter.12.cloned.1.call-update) | async-done | bytes 1179664 | tf_op jit(solution)/shard_map/reduce_scatter | solution.py:211
  670.7 85.5 %reduce-scatter.10.cloned.1.call-done = bf16[768,768]{0,1:T(8,128)(2,1)} async-done(((bf16[3072,768]{0,1:T(8,128)(2,1)}), bf16[768,768]{0,1:T(8,128)(2,1)}) %reduce-scatter.10.cloned.1.call-update) | async-done | bytes 1179664 | tf_op jit(solution)/shard_map/reduce_scatter | solution.py:192
  763.1 90.0 %all-gather.11.cloned.1.call-done = bf16[3072,768]{0,1:T(8,128)(2,1)} async-done(((bf16[768,768]{0,1:T(8,128)(2,1)}), bf16[3072,768]{0,1:T(8,128)(2,1)}) %all-gather.11.cloned.1.call-update) | async-done | bytes 4718608 | tf_op jit(solution)/shard_map/all_gather | solution.py:225
  920.1 83.6 %reduce-scatter.14.cloned.1.call-done = bf16[768,768]{0,1:T(8,128)(2,1)} async-done(((bf16[3072,768]{0,1:T(8,128)(2,1)}), bf16[768,768]{0,1:T(8,128)(2,1)}) %reduce-scatter.14.cloned.1.call-update) | async-done | bytes 1179664 | tf_op jit(solution)/shard_map/reduce_scatter | solution.py:267
  1010.8 8.5 convolution_bitcast_fusion
  1019.3 9.7 copy.144
  1029.6 9.0 fusion.117
  1038.6 9.6 fusion.118
  1050.8 14.8 %all-reduce.4 = (f32[2,192]{1,0:T(2,128)}, f32[768]{0:T(1024)}) all-reduce(f32[2,192]{1,0:T(2,128)S(1)} %pad_maximum_fusion.2, f32[768]{0:T(1024)S(1)} %get-tuple-element.102), channel_id=1, replica_groups=mesh['dp'=8,'mp'=4] {'dp'}, use_global_device_ids=true, to_apply=%region_38.39 | all-reduce | flops 1152 | bytes 9216 | tf_op jit(solution)/shard_map/psum | solution.py:319
  1070.8 8.1 fusion.34
  1080.2 9.6 fusion.36
  1089.9 75.9 %reduce-scatter.16.cloned.1.call-done = f32[96,768]{1,0:T(8,128)} async-done(((f32[3072,768]{1,0:T(8,128)}), f32[96,768]{1,0:T(8,128)}) %reduce-scatter.16.cloned.1.call-update) | async-done | bytes 294928 | tf_op jit(solution)/shard_map/reduce_scatter | solution.py:283
  1168.1 41.6 %all-reduce.3 = (f32[12,128]{1,0:T(8,128)S(1)}, f32[768]{0:T(1024)S(1)}, f32[768]{0:T(1024)}, f32[768]{0:T(1024)}, f32[768]{0:T(1024)}, /*index=5*/f32[768]{0:T(1024)}, f32[768]{0:T(1024)}, f32[768]{0:T(1024)}) all-reduce(f32[12,128]{1,0:T(8,128)S(1)} %convolution_bitcast_fusion.6, ...), channel_id=1, replica_groups=mesh['dp'=8,'mp'=4] {'dp','mp'}, use_global_device_ids=true, to_apply=%region_23.24 | all-reduce | flops 6912 | bytes 55296 | tf_op jit(solution)/shard_map/psum | solution.py:302
  1230.4 52.4 %all-reduce.8.cloned.1.call-done = (f32[768,3,192]{0,2,1:T(8,128)}, f32[192,768]{1,0:T(8,128)}, f32[768,768]{1,0:T(8,128)}, f32[768,768]{1,0:T(8,128)}) async-done(((f32[768,3,192]{0,2,1:T(8,128)}, f32[192,768]{1,0:T(8,128)}, f32[768,768]{1,0:T(8,128)}, f32[768,768]{1,0:T(8,128)}), (f32[768,3,192]{0,2,1:T(8,128)}, f32[192,768]{1,0:T(8,128)}, f32[768,768]{1,0:T(8,128)}, ...) | async-done | bytes 7077904 | tf_op jit(solution)/shard_map/psum | solution.py:319
  (329 shorter events, 222.1 us)
Async XLA Ops:
  7.2 76.9 %all-gather.5.cloned.1.call-start = ((), (), s32[]{:S(2)}) async-start(), calls=%async_computation.5 | async-start | bytes 4866048 | tf_op jit(solution)/shard_map/all_gather | solution.py:122
  17.7 344.8 %reduce-scatter.8.cloned.1.call-start = ((), (), s32[]{:S(2)}) async-start(), calls=%async_computation.6 | async-start | bytes 5898240 | tf_op jit(solution)/shard_map/reduce_scatter | solution.py:178
  93.8 28.3 %collective-permute-start = (bf16[768,768]{0,1:T(8,128)(2,1)S(1)}, bf16[768,768]{0,1:T(8,128)(2,1)}, u32[]{:S(2)}, u32[]{:S(2)}) collective-permute-start(bf16[768,768]{0,1:T(8,128)(2,1)S(1)} %add_convert_fusion.3), channel_id=1, source_target_pairs={{0,1},{1,0},{2,3},{3,2},{4,5},{5,4},{6,7},{7,6},{8,9},{9,8},{10,11... | collective-permute-start | bytes 3538952 | tf_op jit(solution)/shard_map/ppermute | solution.py:139
  125.4 104.3 %collective-permute-start.1 = (bf16[1536,768]{0,1:T(8,128)(2,1)}, bf16[1536,768]{0,1:T(8,128)(2,1)}, u32[]{:S(2)}, u32[]{:S(2)}) collective-permute-start(bf16[1536,768]{0,1:T(8,128)(2,1)} %maximum_select_fusion.1), channel_id=1, source_target_pairs={{0,2},{1,3},{2,0},{3,1},{4,6},{5,7},{6,4},{7,5},{8,10},{9,11},{10,... | collective-permute-start | bytes 7077896 | tf_op jit(solution)/shard_map/ppermute | solution.py:139
  278.8 179.0 %all-gather.7.cloned.1.call-start = ((), (), s32[]{:S(2)}) async-start(), calls=%async_computation.7 | async-start | bytes 5898240 | tf_op jit(solution)/shard_map/all_gather | solution.py:189
  367.7 179.9 %all-gather.9.cloned.1.call-start = ((), (), s32[]{:S(2)}) async-start(), calls=%async_computation.9 | async-start | bytes 5898240 | tf_op jit(solution)/shard_map/all_gather | solution.py:202
  370.8 296.8 %reduce-scatter.12.cloned.1.call-start = ((), (), s32[]{:S(2)}) async-start(), calls=%async_computation.10 | async-start | bytes 5898240 | tf_op jit(solution)/shard_map/reduce_scatter | solution.py:211
  583.8 172.4 %reduce-scatter.10.cloned.1.call-start = ((), (), s32[]{:S(2)}) async-start(), calls=%async_computation.8 | async-start | bytes 5898240 | tf_op jit(solution)/shard_map/reduce_scatter | solution.py:192
  603.8 249.3 %all-gather.11.cloned.1.call-start = ((), (), s32[]{:S(2)}) async-start(), calls=%async_computation.11 | async-start | bytes 5898240 | tf_op jit(solution)/shard_map/all_gather | solution.py:225
  763.0 240.7 %reduce-scatter.14.cloned.1.call-start = ((), (), s32[]{:S(2)}) async-start(), calls=%async_computation.12 | async-start | bytes 5898240 | tf_op jit(solution)/shard_map/reduce_scatter | solution.py:267
  919.8 246.0 %reduce-scatter.16.cloned.1.call-start = ((), (), s32[]{:S(2)}) async-start(), calls=%async_computation.13 | async-start | bytes 9732096 | tf_op jit(solution)/shard_map/reduce_scatter | solution.py:283
  1029.0 253.9 %all-reduce.8.cloned.1.call-start = ((), (), s32[]{:S(2)}) async-start(), calls=%async_computation.14 | async-start | bytes 14155776 | tf_op jit(solution)/shard_map/psum | solution.py:319
  1080.2 129.6 %copy-start.21 = (bf16[128,768]{1,0:T(8,128)(2,1)S(1)}, bf16[128,768]{1,0:T(8,128)(2,1)}, u32[]{:S(2)}) copy-start(bf16[128,768]{1,0:T(8,128)(2,1)} %param.32) | copy-start | bytes 589828
  1080.2 129.8 %copy-start.25 = (f32[12,128]{1,0:T(8,128)S(1)}, f32[12,128]{1,0:T(8,128)}, u32[]{:S(2)}) copy-start(f32[12,128]{1,0:T(8,128)} %copy-done.24) | copy-start | bytes 18436
  1080.2 129.9 %copy-start.54 = (f32[12]{0:T(128)S(1)}, f32[12]{0:T(128)}, u32[]{:S(2)}) copy-start(f32[12]{0:T(128)} %copy-done.53) | copy-start | bytes 148
  1080.2 130.1 %copy-start.77 = (f32[12]{0:T(128)S(1)}, f32[12]{0:T(128)}, u32[]{:S(2)}) copy-start(f32[12]{0:T(128)} %copy-done.76) | copy-start | bytes 148
  1080.2 130.1 %copy-start.58 = (f32[12]{0:T(128)S(1)}, f32[12]{0:T(128)}, u32[]{:S(2)}) copy-start(f32[12]{0:T(128)} %copy-done.57) | copy-start | bytes 148
  1080.2 130.3 %copy-start.37 = (f32[12,2048]{1,0:T(8,128)S(1)}, f32[12,2048]{1,0:T(8,128)}, u32[]{:S(2)}) copy-start(f32[12,2048]{1,0:T(8,128)} %copy-done.36) | copy-start | bytes 294916
  1089.8 123.1 %copy-start.75 = (f32[12]{0:T(128)S(1)}, f32[12]{0:T(128)}, u32[]{:S(2)}) copy-start(f32[12]{0:T(128)} %copy-done.74) | copy-start | bytes 148
  1089.9 123.1 %copy-start.63 = (f32[12]{0:T(128)S(1)}, f32[12]{0:T(128)}, u32[]{:S(2)}) copy-start(f32[12]{0:T(128)} %copy-done.62) | copy-start | bytes 148
  1089.9 123.3 %copy-start.50 = (bf16[128,128]{1,0:T(8,128)(2,1)S(1)}, bf16[128,128]{1,0:T(8,128)(2,1)}, u32[]{:S(2)}) copy-start(bf16[128,128]{1,0:T(8,128)(2,1)} %param.28) | copy-start | bytes 98308
  1089.9 123.6 %copy-start.29 = (f32[4,12,12]{1,2,0:T(8,128)S(1)}, f32[4,12,12]{1,2,0:T(8,128)}, u32[]{:S(2)}) copy-start(f32[4,12,12]{1,2,0:T(8,128)} %copy-done.28) | copy-start | bytes 6916
  1089.9 123.6 %copy-start.35 = (f32[12,1,4,32]{3,2,1,0:T(4,128)S(1)}, f32[12,1,4,32]{3,2,1,0:T(4,128)}, u32[]{:S(2)}) copy-start(f32[12,1,4,32]{3,2,1,0:T(4,128)} %copy-done.34) | copy-start | bytes 18436
  1089.9 123.6 %copy-start.52 = (f32[4,12]{1,0:T(4,128)S(1)}, f32[4,12]{1,0:T(4,128)}, u32[]{:S(2)}) copy-start(f32[4,12]{1,0:T(4,128)} %copy-done.51) | copy-start | bytes 580
  (72 other events, 1138.7 us)
Sparse Core Ops, SparseCore 0:
  17.8 66.2 all-gather.4
  278.9 83.5 reduce-scatter.7
  367.8 89.9 all-gather.6
  459.8 87.7 all-gather.8
  583.9 83.6 reduce-scatter.11
  670.4 85.7 reduce-scatter.9
  763.2 89.8 all-gather.10
  920.0 83.6 reduce-scatter.13
  1029.1 136.6 reduce-scatter.15
  1170.5 112.2 all-reduce.7
